TPU v7x, 32 devices: a whole 2x2x4 slice. The times are simulated.
32 devices in a mesh: grp: 2 (over core), tab: 16 (over z, y, x).
Axes of the slice: x: 2, y: 2, z: 4, core: 2. Of those that a mesh axis runs over, the one named last changes fastest.
Arguments:
- sample_ids: int32 [4, 1024, 1024], P(None, ('grp', 'tab')), may hold values from 0 to 1535
- id_weights: bfloat16 [4, 1024, 1024], P(None, ('grp', 'tab')), may hold values from 0.25 to 2
- dense_features: bfloat16 [4, 1024, 128], P(None, ('grp', 'tab')), may hold values from -6 to 6
- click_labels: int32 [4, 1024], P(None, ('grp', 'tab')), may hold values 0 or 1
- table_shards: bfloat16 [128, 1536, 128], P('tab'), may hold values from -1.1953125 to 1.1953125
- slot_table: int32 [128], replicated, may hold values from 0 to 127, each once
- top_weight: bfloat16 [128, 1024], replicated, may hold values from -0.5 to 0.5
- top_bias: float32 [1024], replicated, may hold values from -3 to 3
- out_weight: bfloat16 [1024], replicated, may hold values from -0.1875 to 0.1875
Outputs:
- logits: float32 [4, 1024], P(None, ('grp', 'tab'))
- grad_top: float32 [128, 1024], replicated
- grad_bias: float32 [1024], replicated
Inputs may be any that keep to these rules, and one draw needn't show every extreme that they name: `slot_table`: a permutation: each table stands in exactly one slot.
All inputs are finite; a program needn't handle non-finite values. No bound on the sum of `click_labels` on one device may be relied on, other than what follows from the above.
Results may differ from a plain program's by a relative error of at most 0.0056.
Values may be sent and summed in bfloat16 or wider, within the bound.
No kernel may reach another device: no remote copies, remote signals or barrier semaphores. Data moves between devices by JAX's collectives and lax.ppermute only.
A program may use at most 128 MiB of HBM per device.

v0:
```python
import functools
import math

import jax
import jax.numpy as jnp
from jax import lax
from jax.experimental import pallas as pl
from jax.experimental.pallas import tpu as pltpu
from jax.sharding import PartitionSpec as P

HOTS = 8
LOSS_SCALE = 32768.0
LANES = 128
SUB = 16
NT = (((1,), (1,)), ((), ()))


def pack_kernel(ids_ref, weights_ref, features_ref, labels_ref, rows_ref, out_ref, *, high, slots):
    members = out_ref.shape[0]
    columns = ids_ref.shape[1]
    block = slots * HOTS
    ids = ids_ref[...].astype(jnp.float32)
    tile = jnp.floor((ids + 0.5) * (1.0 / (SUB * high)))
    rest = ids - tile * (SUB * high)
    hi = jnp.floor((rest + 0.5) * (1.0 / SUB))
    code = rest - hi * SUB + tile * SUB + 128.0
    for bit in (1, 2, 4, 8):
        half = jnp.floor(hi * 0.5)
        code = jnp.where(hi - 2.0 * half > 0.5, code * float(2**bit), code)
        hi = half
    code = code.astype(jnp.bfloat16)
    weights = weights_ref[...]
    eye_r = lax.broadcasted_iota(jnp.int32, (LANES, LANES), 0)
    eye_c = lax.broadcasted_iota(jnp.int32, (LANES, LANES), 1)
    eye = jnp.where(eye_r == eye_c, 1.0, 0.0).astype(jnp.bfloat16)
    turned = lax.dot_general(eye, features_ref[...], NT, preferred_element_type=jnp.float32)
    turned = turned.astype(jnp.bfloat16)
    labels = labels_ref[...].astype(jnp.bfloat16)
    column = lax.broadcasted_iota(jnp.int32, (block, columns), 1)
    for member in range(members):
        rows = rows_ref[member * block : (member + 1) * block, :]
        pick = jnp.where(rows == column, 1.0, 0.0).astype(jnp.bfloat16)
        out_ref[member, 0:block, :] = lax.dot_general(
            pick, code, NT, preferred_element_type=jnp.float32
        ).astype(jnp.bfloat16)
        out_ref[member, block : 2 * block, :] = lax.dot_general(
            pick, weights, NT, preferred_element_type=jnp.float32
        ).astype(jnp.bfloat16)
        out_ref[member, 2 * block : 2 * block + LANES, :] = turned
        out_ref[member, 2 * block + LANES :, :] = labels


def pool_kernel(recv_ref, table_ref, out_ref, hi_ref, lo_ref, w_ref, part_ref, count_ref, acc_ref, *, high, slots, scale):
    slot = pl.program_id(0)
    members = recv_ref.shape[0]
    block = slots * HOTS
    tiles = 128 // SUB

    @pl.when(slot == 0)
    def _():
        def decode(src, carry):
            value = recv_ref[src, 0:block, :].astype(jnp.float32)
            hi = jnp.zeros_like(value)
            for bit in (8, 4, 2, 1):
                big = value >= 128.0 * 2.0**bit
                value = jnp.where(big, value * 2.0**-bit, value)
                hi = jnp.where(big, hi + float(bit), hi)
            hi_ref[src] = hi
            lo_ref[src] = value - 128.0
            w_ref[src] = recv_ref[src, block : 2 * block, :].astype(jnp.float32)
            return carry

        lax.fori_loop(0, members, decode, 0)

    iota = lax.broadcasted_iota(jnp.int32, (SUB, LANES), 0).astype(jnp.float32).astype(jnp.bfloat16)
    zero = jnp.zeros((SUB, LANES), jnp.bfloat16)
    first = pl.multiple_of(slot * HOTS, HOTS)

    def spread(row):
        return jnp.broadcast_to(row, (SUB, LANES)).astype(jnp.bfloat16)

    def pair(index, carry):
        for side in range(2):
            src = index * 2 + side
            hi8 = hi_ref[src, pl.ds(first, HOTS), :]
            lo8 = lo_ref[src, pl.ds(first, HOTS), :]
            w8 = w_ref[src, pl.ds(first, HOTS), :]
            lows = []
            for hot in range(HOTS):
                hi_b = spread(hi8[hot : hot + 1])
                w_b = spread(w8[hot : hot + 1])
                lows.append(spread(lo8[hot : hot + 1]))
                for k in range(high):
                    part_ref[side, hot * high + k] = jnp.where(hi_b == jnp.bfloat16(k), w_b, zero)
            for tile in range(tiles):
                here = iota + jnp.bfloat16(tile * SUB)
                masks = [low == here for low in lows]
                for k in range(high):
                    total = jnp.where(masks[0], part_ref[side, k], zero)
                    for hot in range(1, HOTS):
                        total = total + jnp.where(masks[hot], part_ref[side, hot * high + k], zero)
                    base = (tile * high + k) * SUB
                    count_ref[base : base + SUB, side * LANES : (side + 1) * LANES] = total
        pooled = jnp.dot(table_ref[0], count_ref[...], preferred_element_type=jnp.float32)
        pooled = pooled.astype(jnp.bfloat16).astype(jnp.float32)
        for side in range(2):
            src = index * 2 + side
            turned = recv_ref[src, 2 * block : 2 * block + LANES, :].astype(jnp.float32)
            dots = jnp.sum(pooled[:, side * LANES : (side + 1) * LANES] * turned, axis=0, keepdims=True)
            acc_ref[src, pl.ds(slot, 1), :] = dots * scale
        return carry

    lax.fori_loop(0, members // 2, pair, 0)

    @pl.when(slot == slots - 1)
    def _():
        for src in range(members):
            out_ref[:, src * LANES : (src + 1) * LANES] = acc_ref[src].astype(jnp.bfloat16)


def top_kernel(scores_ref, labels_ref, place_ref, weight_ref, bias_ref, wide_ref, narrow_ref, logits_ref, grad_ref, slope_ref, bias_b, wide_b, *, factor):
    hidden_size = weight_ref.shape[0]
    chunk = 256
    samples = 2 * LANES

    @pl.when(pl.program_id(0) == 0)
    def _():
        grad_ref[...] = jnp.zeros_like(grad_ref)
        bias_b[...] = jnp.broadcast_to(bias_ref[...], bias_b.shape)
        wide_b[...] = jnp.broadcast_to(wide_ref[...], wide_b.shape)

    scores = jnp.dot(place_ref[...], scores_ref[...], preferred_element_type=jnp.float32)
    scores = scores.astype(jnp.bfloat16)
    logits = jnp.zeros((8, samples), jnp.float32)
    for start in range(0, hidden_size, chunk):
        span = slice(start, start + chunk)
        bias = jnp.concatenate([bias_b[span, :]] * 2, axis=1)
        wide = jnp.concatenate([wide_b[span, :]] * 2, axis=1)
        pre = jnp.dot(weight_ref[span, :], scores, preferred_element_type=jnp.float32) + bias
        gate = 0.5 + 0.5 * jnp.tanh(0.5 * pre)
        hidden = pre * gate
        logits = logits + jnp.dot(
            narrow_ref[:, span], hidden.astype(jnp.bfloat16), preferred_element_type=jnp.float32
        )
        slope_ref[span, :] = wide * (gate + hidden * (1.0 - gate))
    logits_ref[...] = logits
    labels = jnp.concatenate([labels_ref[0, 0:1, :], labels_ref[1, 0:1, :]], axis=1)
    delta = (0.5 + 0.5 * jnp.tanh(0.5 * logits[0:1, :]) - labels.astype(jnp.float32)) * factor
    ones = jnp.ones((SUB, samples), jnp.bfloat16)
    left = jnp.concatenate([scores, ones], axis=0)
    for start in range(0, hidden_size, chunk):
        span = slice(start, start + chunk)
        hidden_grad = (slope_ref[span, :] * delta).astype(jnp.bfloat16)
        grad_ref[:, span] += lax.dot_general(left, hidden_grad, NT, preferred_element_type=jnp.float32)


def per_device(
    sample_ids,
    id_weights,
    dense_features,
    click_labels,
    table_shards,
    slot_table,
    top_weight,
    top_bias,
    out_weight,
):
    micro, local_batch, columns = sample_ids.shape
    tables = slot_table.shape[0]
    slots, vocab, width = table_shards.shape
    hidden_size = top_weight.shape[1]
    members = lax.axis_size("tab")
    groups = lax.axis_size("grp")
    local = micro * local_batch
    high = vocab // 128
    assert local == LANES and width == LANES and vocab % 128 == 0 and high <= 16 and members % 2 == 0
    block = slots * HOTS
    height = 2 * block + LANES + SUB
    scale = 1.0 / math.sqrt(width)

    rows = (slot_table[:, None] * HOTS + jnp.arange(HOTS, dtype=jnp.int32)[None, :]).reshape(columns, 1)
    labels = jnp.broadcast_to(click_labels.reshape(1, local), (SUB, local)).astype(jnp.float32)
    packed = pl.pallas_call(
        functools.partial(pack_kernel, high=high, slots=slots),
        out_shape=jax.ShapeDtypeStruct((members, height, LANES), jnp.bfloat16),
        name="pack",
    )(
        sample_ids.reshape(local, columns),
        id_weights.reshape(local, columns),
        dense_features.reshape(local, width),
        labels,
        rows,
    )
    received = lax.all_to_all(packed, "tab", split_axis=0, concat_axis=0, tiled=True)
    turned_tables = jnp.swapaxes(table_shards, 1, 2)
    samples = members * LANES
    scores = pl.pallas_call(
        functools.partial(pool_kernel, high=high, slots=slots, scale=scale),
        grid=(slots,),
        in_specs=[
            pl.BlockSpec((members, height, LANES), lambda s: (0, 0, 0)),
            pl.BlockSpec((1, width, vocab), lambda s: (s, 0, 0)),
        ],
        out_specs=pl.BlockSpec((slots, samples), lambda s: (0, 0)),
        out_shape=jax.ShapeDtypeStruct((slots, samples), jnp.bfloat16),
        scratch_shapes=[
            pltpu.VMEM((members, block, LANES), jnp.float32),
            pltpu.VMEM((members, block, LANES), jnp.float32),
            pltpu.VMEM((members, block, LANES), jnp.float32),
            pltpu.VMEM((2, HOTS * high, SUB, LANES), jnp.bfloat16),
            pltpu.VMEM((vocab, 2 * LANES), jnp.bfloat16),
            pltpu.VMEM((members, slots, LANES), jnp.float32),
        ],
        name="pool",
    )(received, turned_tables)
    gathered = lax.all_gather(scores, "tab", axis=0, tiled=True)
    place = (jnp.arange(tables, dtype=jnp.int32)[:, None] == slot_table[None, :]).astype(jnp.bfloat16)
    label_block = (2 * block + LANES) // SUB
    logits, grad = pl.pallas_call(
        functools.partial(top_kernel, factor=LOSS_SCALE / (local * members * groups)),
        grid=(members // 2,),
        in_specs=[
            pl.BlockSpec((tables, 2 * LANES), lambda j: (0, j)),
            pl.BlockSpec((2, SUB, LANES), lambda j: (j, label_block, 0)),
            pl.BlockSpec((tables, tables), lambda j: (0, 0)),
            pl.BlockSpec((hidden_size, tables), lambda j: (0, 0)),
            pl.BlockSpec((hidden_size, 1), lambda j: (0, 0)),
            pl.BlockSpec((hidden_size, 1), lambda j: (0, 0)),
            pl.BlockSpec((8, hidden_size), lambda j: (0, 0)),
        ],
        out_specs=[
            pl.BlockSpec((8, 2 * LANES), lambda j: (0, j)),
            pl.BlockSpec((tables + SUB, hidden_size), lambda j: (0, 0)),
        ],
        out_shape=[
            jax.ShapeDtypeStruct((8, samples), jnp.float32),
            jax.ShapeDtypeStruct((tables + SUB, hidden_size), jnp.float32),
        ],
        scratch_shapes=[
            pltpu.VMEM((hidden_size, 2 * LANES), jnp.float32),
            pltpu.VMEM((hidden_size, LANES), jnp.float32),
            pltpu.VMEM((hidden_size, LANES), jnp.float32),
        ],
        name="top",
    )(
        gathered,
        received,
        place,
        top_weight.T,
        top_bias.reshape(hidden_size, 1),
        out_weight.astype(jnp.float32).reshape(hidden_size, 1),
        jnp.broadcast_to(out_weight[None, :], (8, hidden_size)),
    )
    if groups == 2:
        grad = grad + lax.ppermute(grad, "grp", [(0, 1), (1, 0)])
    else:
        grad = lax.psum(grad, "grp")
    own = lax.dynamic_slice(logits, (0, lax.axis_index("tab") * LANES), (1, LANES))
    return own.reshape(micro, local_batch), grad[:tables], grad[tables]


def solution(mesh):
    return jax.shard_map(
        per_device,
        mesh=mesh,
        in_specs=(
            P(None, ("grp", "tab"), None),
            P(None, ("grp", "tab"), None),
            P(None, ("grp", "tab"), None),
            P(None, ("grp", "tab")),
            P("tab", None, None),
            P(),
            P(),
            P(),
            P(),
        ),
        out_specs=(P(None, ("grp", "tab")), P(), P()),
        check_vma=False,
    )
```

profile of v0, /device:TPU:0, one launch (start us, length us, event | category | flops | bytes accessed | tf_op | source)
XLA Modules:
  0.0 180.2 jit_solution(4263084177511146346)
XLA Ops:
  0.6 0.7 broadcast_multiply_fusion
  1.4 1.0 add.35.rows_ref
  2.4 0.7 convert_element_type.9
  3.0 0.1 convert_element_type.10
  3.1 0.6 broadcast_in_dim.4.labels_ref
  3.7 5.6 %pack.1 = bf16[16,272,128]{2,1,0:T(8,128)(2,1)} custom-call(s32[128,1024]{1,0:T(8,128)} %bitcast.10, bf16[128,1024]{1,0:T(8,128)(2,1)} %bitcast.11, bf16[128,128]{1,0:T(8,128)(2,1)} %bitcast.12, f32[16,128]{1,0:T(8,128)} %broadcast_in_dim.4.labels_ref, s32[1024,1]{1,0:T(8,128)} %add.35.rows_ref), custom_call_target="tpu_custom_call" | custom-call | tf_op jit(solution)/shard_map/pack/pallas_call | solution.py:183
  9.4 8.3 %all-to-all-start = ((bf16[16,272,128]{2,1,0:T(8,128)(2,1)}), bf16[16,272,128]{2,1,0:T(8,128)(2,1)S(1)}, u32[]{:S(2)}, u32[]{:S(2)}) async-start(bf16[16,272,128]{2,1,0:T(8,128)(2,1)} %pack.1), calls=%async_computation | async-start | bytes 2228224 | tf_op jit(solution)/shard_map/all_to_all | solution.py:194
  17.8 4.7 %copy.15 = bf16[8,1536,128]{1,2,0:T(8,128)(2,1)} copy(bf16[8,1536,128]{2,1,0:T(8,128)(2,1)} %param.13) | data formatting | bytes 6291456 | tf_op args[4]
  22.5 1.0 copy.18.wide_ref
  23.5 1.0 copy.17.bias_ref
  24.6 0.8 copy.16
  25.4 0.6 fusion.place_ref
  26.0 17.4 %all-to-all-done.recv_ref.labels_ref = bf16[16,272,128]{2,1,0:T(8,128)(2,1)S(1)} async-done(((bf16[16,272,128]{2,1,0:T(8,128)(2,1)}), bf16[16,272,128]{2,1,0:T(8,128)(2,1)S(1)}, u32[]{:S(2)}, u32[]{:S(2)}) %all-to-all-start) | async-done | bytes 1114144 | tf_op jit(solution)/shard_map/all_to_all | solution.py:194
  43.4 1.0 copy-done
  44.4 71.2 %pool.1 = bf16[8,2048]{1,0:T(8,128)(2,1)} custom-call(bf16[16,272,128]{2,1,0:T(8,128)(2,1)} %copy-done, bf16[8,128,1536]{2,1,0:T(8,128)(2,1)} %bitcast.8), custom_call_target="tpu_custom_call" | custom-call | tf_op jit(solution)/shard_map/pool/pallas_call | solution.py:197
  115.6 45.9 %all_gather.3.scores_ref = bf16[128,2048]{1,0:T(8,128)(2,1)} all-gather(bf16[8,2048]{1,0:T(8,128)(2,1)} %pool.1), channel_id=1, replica_groups=mesh['grp'=2,'tab'=16] {'tab'}, dimensions={0}, use_global_device_ids=true | all-gather | bytes 557056 | tf_op jit(solution)/shard_map/all_gather | solution.py:216
  161.5 0.6 broadcast_in_dim.5.narrow_ref
  162.1 13.3 %top.1 = (f32[8,2048]{1,0:T(8,128)}, f32[144,1024]{1,0:T(8,128)}) custom-call(bf16[128,2048]{1,0:T(8,128)(2,1)} %all_gather.3.scores_ref, bf16[16,272,128]{2,1,0:T(8,128)(2,1)} %copy-done, bf16[128,128]{1,0:T(8,128)(2,1)} %fusion.place_ref, bf16[1024,128]{1,0:T(8,128)(2,1)} %bitcast.9, f32[1024,1]{1,0:T(8,128)} %copy.17.bias_ref, f32[1024,1]{1,0:T(8,128)} %copy.18.wide_ref, ...), custom_call_target="tpu_custom_call" | custom-call | tf_op jit(solution)/shard_map/top/pallas_call | solution.py:219
  175.4 0.7 dynamic-slice_reduce_fusion
  176.1 0.7 reshape.62
  176.8 0.8 collective-permute-done
  177.6 1.1 add.34
  178.8 0.8 slice.8
  179.6 0.6 slice.9
  (12 shorter events, 0.1 us)
Async XLA Ops:
  9.4 34.0 %all-to-all-start = ((bf16[16,272,128]{2,1,0:T(8,128)(2,1)}), bf16[16,272,128]{2,1,0:T(8,128)(2,1)S(1)}, u32[]{:S(2)}, u32[]{:S(2)}) async-start(bf16[16,272,128]{2,1,0:T(8,128)(2,1)} %pack.1), calls=%async_computation | async-start | bytes 2228224 | tf_op jit(solution)/shard_map/all_to_all | solution.py:194
  17.7 4.8 %copy-start.2 = (bf16[1024]{0:T(1024)(128)(2,1)S(1)}, bf16[1024]{0:T(1024)(128)(2,1)}, u32[]{:S(2)}) copy-start(bf16[1024]{0:T(1024)(128)(2,1)} %param.17) | copy-start | bytes 6148
  17.7 5.8 %copy-start.3 = (f32[1024]{0:T(1024)S(1)}, f32[1024]{0:T(1024)}, u32[]{:S(2)}) copy-start(f32[1024]{0:T(1024)} %param.16) | copy-start | bytes 12292
  17.8 6.8 %copy-start.1 = (bf16[128,1024]{1,0:T(8,128)(2,1)S(1)}, bf16[128,1024]{1,0:T(8,128)(2,1)}, u32[]{:S(2)}) copy-start(bf16[128,1024]{1,0:T(8,128)(2,1)} %param.15) | copy-start | bytes 786436
  17.8 7.6 %copy-start.4 = (s32[128]{0:T(128)S(1)}, s32[128]{0:T(128)}, u32[]{:S(2)}) copy-start(s32[128]{0:T(128)} %param.14) | copy-start | bytes 1540
  43.4 1.0 copy-start
  175.4 2.2 %collective-permute-start = (f32[144,1024]{1,0:T(8,128)}, f32[144,1024]{1,0:T(8,128)S(1)}, u32[]{:S(2)}, u32[]{:S(2)}) collective-permute-start(f32[144,1024]{1,0:T(8,128)} %get-tuple-element.6), channel_id=1, source_target_pairs={{0,16},{16,0},{1,17},{17,1},{2,18},{18,2},{3,19},{19,3},{4,20},{20... | collective-permute-start | bytes 1769480 | tf_op jit(solution)/shard_map/ppermute | solution.py:255
where the time goes:
time: 181 us; the launch traced here: 180 us
  Pallas kernels  90.2 us (50%)
  blocking collectives  45.9 us (25%)
  waiting for transfers between devices  18.2 us (10%)
  local copies, waits for them, and re-layouts  13.7 us (8%)
  starting transfers between devices  8.35 us (5%)
  other arithmetic  3.18 us (2%)
    pallas_call x1, Pallas kernels, per_device(): pl.pallas_call(functools.partial(pool_kernel, high=high, slots=slots, sca...  71.2 us
    all_gather x1, blocking collectives, per_device(): gathered = lax.all_gather(scores, 'tab', axis=0, tiled=True)  45.9 us
    all_to_all x1, waiting for transfers between devices, per_device(): lax.all_to_all(packed, 'tab', split_axis=0, concat_axis=0, tiled=True)  17.4 us
    pallas_call x1, Pallas kernels, per_device(): pl.pallas_call(functools.partial(top_kernel, factor=LOSS_SCALE / (local *...  13.3 us
    all_to_all x1, starting transfers between devices, per_device(): lax.all_to_all(packed, 'tab', split_axis=0, concat_axis=0, tiled=True)  8.35 us
    unnamed x12, local copies, waits for them, and re-layouts  6.58 us
    pallas_call x1, Pallas kernels, per_device(): pl.pallas_call(functools.partial(pack_kernel, high=high, slots=slots), ou...  5.64 us
  transfers between devices with their start and end apart: 2, of which 2 were waited for; matrix products, arithmetic and copies ran while one was open for 5% of the time, Pallas kernels for 0%

commit v1 on v0

--- a/solution.py
+++ b/solution.py
@@ -50,11 +50,12 @@
         out_ref[member, 2 * block + LANES :, :] = labels
 
 
-def pool_kernel(recv_ref, table_ref, out_ref, hi_ref, lo_ref, w_ref, part_ref, count_ref, acc_ref, *, high, slots, scale):
+def pool_kernel(recv_ref, table_ref, out_ref, hi_ref, lo_ref, w_ref, part_ref, low_ref, even_ref, odd_ref, sum_ref, acc_ref, *, high, slots, scale):
     slot = pl.program_id(0)
     members = recv_ref.shape[0]
     block = slots * HOTS
-    tiles = 128 // SUB
+    pairs = members // 2
+    steps = even_ref.shape[0]
 
     @pl.when(slot == 0)
     def _():
@@ -72,45 +73,78 @@
 
         lax.fori_loop(0, members, decode, 0)
 
-    iota = lax.broadcasted_iota(jnp.int32, (SUB, LANES), 0).astype(jnp.float32).astype(jnp.bfloat16)
+    iota = lax.broadcasted_iota(jnp.int32, (SUB, LANES), 0).astype(jnp.float32)
     zero = jnp.zeros((SUB, LANES), jnp.bfloat16)
     first = pl.multiple_of(slot * HOTS, HOTS)
 
     def spread(row):
         return jnp.broadcast_to(row, (SUB, LANES)).astype(jnp.bfloat16)
 
-    def pair(index, carry):
+    def count(pair, new_ref, old_ref):
         for side in range(2):
-            src = index * 2 + side
+            src = pair * 2 + side
             hi8 = hi_ref[src, pl.ds(first, HOTS), :]
             lo8 = lo_ref[src, pl.ds(first, HOTS), :]
             w8 = w_ref[src, pl.ds(first, HOTS), :]
-            lows = []
             for hot in range(HOTS):
                 hi_b = spread(hi8[hot : hot + 1])
                 w_b = spread(w8[hot : hot + 1])
-                lows.append(spread(lo8[hot : hot + 1]))
+                low_ref[side, hot] = spread(lo8[hot : hot + 1])
                 for k in range(high):
                     part_ref[side, hot * high + k] = jnp.where(hi_b == jnp.bfloat16(k), w_b, zero)
-            for tile in range(tiles):
-                here = iota + jnp.bfloat16(tile * SUB)
-                masks = [low == here for low in lows]
-                for k in range(high):
-                    total = jnp.where(masks[0], part_ref[side, k], zero)
-                    for hot in range(1, HOTS):
-                        total = total + jnp.where(masks[hot], part_ref[side, hot * high + k], zero)
-                    base = (tile * high + k) * SUB
-                    count_ref[base : base + SUB, side * LANES : (side + 1) * LANES] = total
-        pooled = jnp.dot(table_ref[0], count_ref[...], preferred_element_type=jnp.float32)
-        pooled = pooled.astype(jnp.bfloat16).astype(jnp.float32)
+        if old_ref is not None:
+            sum_ref[...] = jnp.zeros_like(sum_ref)
+
+        def step(q, carry):
+            if old_ref is not None:
+                sum_ref[...] += jnp.dot(table_ref[0, q], old_ref[q], preferred_element_type=jnp.float32)
+            start = (q * (2 * SUB)).astype(jnp.float32)
+            here = [(iota + (start + t * SUB)).astype(jnp.bfloat16) for t in range(2)]
+            for side in range(2):
+                totals = [[None] * high for _ in range(2)]
+                for hot in range(HOTS):
+                    low = low_ref[side, hot]
+                    masks = [low == here[t] for t in range(2)]
+                    for k in range(high):
+                        part = part_ref[side, hot * high + k]
+                        for t in range(2):
+                            addend = jnp.where(masks[t], part, zero)
+                            totals[t][k] = addend if hot == 0 else totals[t][k] + addend
+                for t in range(2):
+                    for k in range(high):
+                        base = (t * high + k) * SUB
+                        new_ref[q, base : base + SUB, side * LANES : (side + 1) * LANES] = totals[t][k]
+            return carry
+
+        lax.fori_loop(0, steps, step, 0)
+
+    def finish(pair):
+        pooled = sum_ref[...].astype(jnp.bfloat16).astype(jnp.float32)
         for side in range(2):
-            src = index * 2 + side
+            src = pair * 2 + side
             turned = recv_ref[src, 2 * block : 2 * block + LANES, :].astype(jnp.float32)
             dots = jnp.sum(pooled[:, side * LANES : (side + 1) * LANES] * turned, axis=0, keepdims=True)
             acc_ref[src, pl.ds(slot, 1), :] = dots * scale
+
+    count(0, even_ref, None)
+
+    def two(index, carry):
+        count(2 * index + 1, odd_ref, even_ref)
+        finish(2 * index)
+
+        @pl.when(index < pairs // 2 - 1)
+        def _():
+            count(2 * index + 2, even_ref, odd_ref)
+            finish(2 * index + 1)
+
         return carry
 
-    lax.fori_loop(0, members // 2, pair, 0)
+    lax.fori_loop(0, pairs // 2, two, 0)
+    last = jnp.zeros(sum_ref.shape, jnp.float32)
+    for q in range(steps):
+        last = last + jnp.dot(table_ref[0, q], odd_ref[q], preferred_element_type=jnp.float32)
+    sum_ref[...] = last
+    finish(pairs - 1)
 
     @pl.when(slot == slots - 1)
     def _():
@@ -173,7 +207,7 @@
     groups = lax.axis_size("grp")
     local = micro * local_batch
     high = vocab // 128
-    assert local == LANES and width == LANES and vocab % 128 == 0 and high <= 16 and members % 2 == 0
+    assert local == LANES and width == LANES and vocab % 128 == 0 and high <= 16 and members % 4 == 0
     block = slots * HOTS
     height = 2 * block + LANES + SUB
     scale = 1.0 / math.sqrt(width)
@@ -192,14 +226,15 @@
         rows,
     )
     received = lax.all_to_all(packed, "tab", split_axis=0, concat_axis=0, tiled=True)
-    turned_tables = jnp.swapaxes(table_shards, 1, 2)
+    steps = 128 // (2 * SUB)
+    turned_tables = jnp.swapaxes(table_shards.reshape(slots, steps, vocab // steps, width), 2, 3)
     samples = members * LANES
     scores = pl.pallas_call(
         functools.partial(pool_kernel, high=high, slots=slots, scale=scale),
         grid=(slots,),
         in_specs=[
             pl.BlockSpec((members, height, LANES), lambda s: (0, 0, 0)),
-            pl.BlockSpec((1, width, vocab), lambda s: (s, 0, 0)),
+            pl.BlockSpec((1, steps, width, vocab // steps), lambda s: (s, 0, 0, 0)),
         ],
         out_specs=pl.BlockSpec((slots, samples), lambda s: (0, 0)),
         out_shape=jax.ShapeDtypeStruct((slots, samples), jnp.bfloat16),
@@ -208,12 +243,17 @@
             pltpu.VMEM((members, block, LANES), jnp.float32),
             pltpu.VMEM((members, block, LANES), jnp.float32),
             pltpu.VMEM((2, HOTS * high, SUB, LANES), jnp.bfloat16),
-            pltpu.VMEM((vocab, 2 * LANES), jnp.bfloat16),
+            pltpu.VMEM((2, HOTS, SUB, LANES), jnp.bfloat16),
+            pltpu.VMEM((steps, vocab // steps, 2 * LANES), jnp.bfloat16),
+            pltpu.VMEM((steps, vocab // steps, 2 * LANES), jnp.bfloat16),
+            pltpu.VMEM((width, 2 * LANES), jnp.float32),
             pltpu.VMEM((members, slots, LANES), jnp.float32),
         ],
         name="pool",
     )(received, turned_tables)
-    gathered = lax.all_gather(scores, "tab", axis=0, tiled=True)
+    copies = jnp.broadcast_to(scores[None], (members, slots, samples))
+    gathered = lax.all_to_all(copies, "tab", split_axis=0, concat_axis=0, tiled=True)
+    gathered = gathered.reshape(tables, samples)
     place = (jnp.arange(tables, dtype=jnp.int32)[:, None] == slot_table[None, :]).astype(jnp.bfloat16)
     label_block = (2 * block + LANES) // SUB
     logits, grad = pl.pallas_call(

time: 181 us -> 202 us (1.12)
  blocking collectives: 45.9 us -> 0 us
  Pallas kernels: 90.2 us -> 136 us
  waiting for transfers between devices: 18.2 us -> 32.2 us
  starting transfers between devices: 8.35 us -> 14.3 us
    all_gather x1 -> x0, blocking collectives: 45.9 us -> none  [per_device(): gathered = lax.all_gather(scores, 'tab', axis=0, tiled=True)]
    pallas_call x1, Pallas kernels: 71.2 us -> 117 us  [per_device(): pl.pallas_call(functools.partial(pool_kernel, high=high, slots=slots, sca...]
    all_to_all x0 -> x1, waiting for transfers between devices: none -> 10.3 us  [per_device(): lax.all_to_all(copies, 'tab', split_axis=0, concat_axis=0, tiled=True)]
    all_to_all x0 -> x1, starting transfers between devices: none -> 6 us  [per_device(): lax.all_to_all(copies, 'tab', split_axis=0, concat_axis=0, tiled=True)]
    reshape x0 -> x1, local copies, waits for them, and re-layouts: none -> 4.64 us  [per_device(): table_shards.reshape(slots, steps, vocab // steps, width)]
    unnamed x12 -> x13, local copies, waits for them, and re-layouts: 6.58 us -> 2.02 us
    all_to_all x1, waiting for transfers between devices: 17.4 us -> 21 us  [per_device(): lax.all_to_all(packed, 'tab', split_axis=0, concat_axis=0, tiled=True)]
  transfers between devices with their start and end apart: 2 -> 3, of which waited for: 2 -> 3; matrix products, arithmetic and copies ran while one was open for 5% -> 5% of each run, Pallas kernels for 0% -> 0%
where the time goes in v1:
time: 202 us; the launch traced here: 201 us
  Pallas kernels  136 us (67%)
  waiting for transfers between devices  32.2 us (16%)
  local copies, waits for them, and re-layouts  15.5 us (8%)
  starting transfers between devices  14.3 us (7%)
  other arithmetic  3.17 us (2%)
    pallas_call x1, Pallas kernels, per_device(): pl.pallas_call(functools.partial(pool_kernel, high=high, slots=slots, sca...  117 us
    all_to_all x1, waiting for transfers between devices, per_device(): lax.all_to_all(packed, 'tab', split_axis=0, concat_axis=0, tiled=True)  21 us
    pallas_call x1, Pallas kernels, per_device(): pl.pallas_call(functools.partial(top_kernel, factor=LOSS_SCALE / (local *...  13.3 us
    all_to_all x1, waiting for transfers between devices, per_device(): lax.all_to_all(copies, 'tab', split_axis=0, concat_axis=0, tiled=True)  10.3 us
    all_to_all x1, starting transfers between devices, per_device(): lax.all_to_all(packed, 'tab', split_axis=0, concat_axis=0, tiled=True)  8.34 us
    all_to_all x1, starting transfers between devices, per_device(): lax.all_to_all(copies, 'tab', split_axis=0, concat_axis=0, tiled=True)  6 us
    pallas_call x1, Pallas kernels, per_device(): pl.pallas_call(functools.partial(pack_kernel, high=high, slots=slots), ou...  5.65 us
    reshape x1, local copies, waits for them, and re-layouts, per_device(): table_shards.reshape(slots, steps, vocab // steps, width)  4.64 us
  transfers between devices with their start and end apart: 3, of which 3 were waited for; matrix products, arithmetic and copies ran while one was open for 5% of the time, Pallas kernels for 0%

profile of v1, /device:TPU:0, one launch (start us, length us, event | category | flops | bytes accessed | tf_op | source)
XLA Modules:
  0.0 201.4 jit_solution(14680110872639697991)
XLA Ops:
  0.6 0.7 broadcast_multiply_fusion
  1.4 1.0 add.35.rows_ref
  2.4 0.7 convert_element_type.9
  3.1 0.6 broadcast_in_dim.6.labels_ref
  3.7 5.6 %pack.1 = bf16[16,272,128]{2,1,0:T(8,128)(2,1)} custom-call(s32[128,1024]{1,0:T(8,128)} %bitcast.14, bf16[128,1024]{1,0:T(8,128)(2,1)} %bitcast.15, bf16[128,128]{1,0:T(8,128)(2,1)} %bitcast.16, f32[16,128]{1,0:T(8,128)} %broadcast_in_dim.6.labels_ref, s32[1024,1]{1,0:T(8,128)} %add.35.rows_ref), custom_call_target="tpu_custom_call" | custom-call | tf_op jit(solution)/shard_map/pack/pallas_call | solution.py:217
  9.4 8.3 %all-to-all-start = ((bf16[16,272,128]{2,1,0:T(8,128)(2,1)}), bf16[16,272,128]{2,1,0:T(8,128)(2,1)S(1)}, u32[]{:S(2)}, u32[]{:S(2)}) async-start(bf16[16,272,128]{2,1,0:T(8,128)(2,1)} %pack.1), calls=%async_computation | async-start | bytes 2228224 | tf_op jit(solution)/shard_map/all_to_all | solution.py:228
  17.7 4.6 %copy.14 = bf16[8,4,384,128]{2,3,1,0:T(8,128)(2,1)} copy(bf16[8,4,384,128]{3,2,1,0:T(8,128)(2,1)} %bitcast.11) | data formatting | bytes 6291456 | tf_op jit(solution)/shard_map/reshape | solution.py:230
  22.4 21.0 %all-to-all-done.recv_ref.labels_ref = bf16[16,272,128]{2,1,0:T(8,128)(2,1)S(1)} async-done(((bf16[16,272,128]{2,1,0:T(8,128)(2,1)}), bf16[16,272,128]{2,1,0:T(8,128)(2,1)S(1)}, u32[]{:S(2)}, u32[]{:S(2)}) %all-to-all-start) | async-done | bytes 1114144 | tf_op jit(solution)/shard_map/all_to_all | solution.py:228
  43.4 1.0 copy-done
  44.4 116.6 %pool.1 = bf16[8,2048]{1,0:T(8,128)(2,1)} custom-call(bf16[16,272,128]{2,1,0:T(8,128)(2,1)} %copy-done, bf16[8,4,128,384]{3,2,1,0:T(8,128)(2,1)} %bitcast.10), custom_call_target="tpu_custom_call" | custom-call | tf_op jit(solution)/shard_map/pool/pallas_call | solution.py:232
  161.0 1.6 broadcast_in_dim.7
  162.6 6.0 %all-to-all-start.1 = ((bf16[16,8,2048]{2,1,0:T(8,128)(2,1)}), bf16[16,8,2048]{2,1,0:T(8,128)(2,1)S(1)}, u32[]{:S(2)}, u32[]{:S(2)}) async-start(bf16[16,8,2048]{2,1,0:T(8,128)(2,1)} %broadcast_in_dim.7), calls=%async_computation.1 | async-start | bytes 1048576 | tf_op jit(solution)/shard_map/all_to_all | solution.py:255
  168.6 1.1 copy.17.wide_ref
  169.7 1.0 copy.16.bias_ref
  170.7 0.8 copy.15
  171.6 0.6 fusion.place_ref
  172.2 10.3 %all-to-all-done.1 = bf16[16,8,2048]{2,1,0:T(8,128)(2,1)S(1)} async-done(((bf16[16,8,2048]{2,1,0:T(8,128)(2,1)}), bf16[16,8,2048]{2,1,0:T(8,128)(2,1)S(1)}, u32[]{:S(2)}, u32[]{:S(2)}) %all-to-all-start.1) | async-done | bytes 524320 | tf_op jit(solution)/shard_map/all_to_all | solution.py:255
  182.5 0.6 broadcast_in_dim.8.narrow_ref
  183.3 13.3 %top.1 = (f32[8,2048]{1,0:T(8,128)}, f32[144,1024]{1,0:T(8,128)}) custom-call(bf16[128,2048]{1,0:T(8,128)(2,1)} %bitcast.12, bf16[16,272,128]{2,1,0:T(8,128)(2,1)} %copy-done, bf16[128,128]{1,0:T(8,128)(2,1)} %fusion.place_ref, bf16[1024,128]{1,0:T(8,128)(2,1)} %bitcast.13, f32[1024,1]{1,0:T(8,128)} %copy.16.bias_ref, f32[1024,1]{1,0:T(8,128)} %copy.17.wide_ref, ...), custom_call_target="tpu_custom_call" | custom-call | tf_op jit(solution)/shard_map/top/pallas_call | solution.py:259
  196.6 0.7 dynamic-slice_reduce_fusion
  197.3 0.7 reshape.71
  198.0 0.8 collective-permute-done
  198.8 1.1 add.34
  199.9 0.8 slice.8
  (16 shorter events, 0.9 us)
Async XLA Ops:
  9.4 34.0 %all-to-all-start = ((bf16[16,272,128]{2,1,0:T(8,128)(2,1)}), bf16[16,272,128]{2,1,0:T(8,128)(2,1)S(1)}, u32[]{:S(2)}, u32[]{:S(2)}) async-start(bf16[16,272,128]{2,1,0:T(8,128)(2,1)} %pack.1), calls=%async_computation | async-start | bytes 2228224 | tf_op jit(solution)/shard_map/all_to_all | solution.py:228
  22.4 146.2 %copy-start.3 = (bf16[1024]{0:T(1024)(128)(2,1)S(1)}, bf16[1024]{0:T(1024)(128)(2,1)}, u32[]{:S(2)}) copy-start(bf16[1024]{0:T(1024)(128)(2,1)} %param.17) | copy-start | bytes 6148
  43.4 1.0 copy-start
  44.4 125.3 %copy-start.4 = (f32[1024]{0:T(1024)S(1)}, f32[1024]{0:T(1024)}, u32[]{:S(2)}) copy-start(f32[1024]{0:T(1024)} %param.16) | copy-start | bytes 12292
  44.4 126.3 %copy-start.2 = (bf16[128,1024]{1,0:T(8,128)(2,1)S(1)}, bf16[128,1024]{1,0:T(8,128)(2,1)}, u32[]{:S(2)}) copy-start(bf16[128,1024]{1,0:T(8,128)(2,1)} %param.15) | copy-start | bytes 786436
  44.4 127.1 %copy-start.5 = (s32[128]{0:T(128)S(1)}, s32[128]{0:T(128)}, u32[]{:S(2)}) copy-start(s32[128]{0:T(128)} %param.14) | copy-start | bytes 1540
  162.6 19.9 %all-to-all-start.1 = ((bf16[16,8,2048]{2,1,0:T(8,128)(2,1)}), bf16[16,8,2048]{2,1,0:T(8,128)(2,1)S(1)}, u32[]{:S(2)}, u32[]{:S(2)}) async-start(bf16[16,8,2048]{2,1,0:T(8,128)(2,1)} %broadcast_in_dim.7), calls=%async_computation.1 | async-start | bytes 1048576 | tf_op jit(solution)/shard_map/all_to_all | solution.py:255
  182.5 0.8 copy-start.1
  196.6 2.2 %collective-permute-start = (f32[144,1024]{1,0:T(8,128)}, f32[144,1024]{1,0:T(8,128)S(1)}, u32[]{:S(2)}, u32[]{:S(2)}) collective-permute-start(f32[144,1024]{1,0:T(8,128)} %get-tuple-element.6), channel_id=1, source_target_pairs={{0,16},{16,0},{1,17},{17,1},{2,18},{18,2},{3,19},{19,3},{4,20},{20... | collective-permute-start | bytes 1769480 | tf_op jit(solution)/shard_map/ppermute | solution.py:295

commit v2 on v0

--- a/solution.py
+++ b/solution.py
@@ -213,7 +213,9 @@
         ],
         name="pool",
     )(received, turned_tables)
-    gathered = lax.all_gather(scores, "tab", axis=0, tiled=True)
+    copies = jnp.broadcast_to(scores[None], (members, slots, samples))
+    gathered = lax.all_to_all(copies, "tab", split_axis=0, concat_axis=0, tiled=True)
+    gathered = gathered.reshape(tables, samples)
     place = (jnp.arange(tables, dtype=jnp.int32)[:, None] == slot_table[None, :]).astype(jnp.bfloat16)
     label_block = (2 * block + LANES) // SUB
     logits, grad = pl.pallas_call(

time: 181 us -> 157 us (0.87)
  blocking collectives: 45.9 us -> 0 us
  waiting for transfers between devices: 18.2 us -> 32.2 us
  starting transfers between devices: 8.35 us -> 14.3 us
    all_gather x1 -> x0, blocking collectives: 45.9 us -> none  [per_device(): gathered = lax.all_gather(scores, 'tab', axis=0, tiled=True)]
    all_to_all x0 -> x1, waiting for transfers between devices: none -> 10.3 us  [per_device(): lax.all_to_all(copies, 'tab', split_axis=0, concat_axis=0, tiled=True)]
    all_to_all x0 -> x1, starting transfers between devices: none -> 6 us  [per_device(): lax.all_to_all(copies, 'tab', split_axis=0, concat_axis=0, tiled=True)]
    all_to_all x1, waiting for transfers between devices: 17.4 us -> 21 us  [per_device(): lax.all_to_all(packed, 'tab', split_axis=0, concat_axis=0, tiled=True)]
    unnamed x12 -> x14, local copies, waits for them, and re-layouts: 6.58 us -> 6.66 us
  transfers between devices with their start and end apart: 2 -> 3, of which waited for: 2 -> 3; matrix products, arithmetic and copies ran while one was open for 5% -> 6% of each run, Pallas kernels for 0% -> 0%
where the time goes in v2:
time: 157 us; the launch traced here: 156 us
  Pallas kernels  90.2 us (57%)
  waiting for transfers between devices  32.2 us (21%)
  local copies, waits for them, and re-layouts  15.5 us (10%)
  starting transfers between devices  14.3 us (9%)
  other arithmetic  3.17 us (2%)
    pallas_call x1, Pallas kernels, per_device(): pl.pallas_call(functools.partial(pool_kernel, high=high, slots=slots, sca...  71.3 us
    all_to_all x1, waiting for transfers between devices, per_device(): lax.all_to_all(packed, 'tab', split_axis=0, concat_axis=0, tiled=True)  21 us
    pallas_call x1, Pallas kernels, per_device(): pl.pallas_call(functools.partial(top_kernel, factor=LOSS_SCALE / (local *...  13.3 us
    all_to_all x1, waiting for transfers between devices, per_device(): lax.all_to_all(copies, 'tab', split_axis=0, concat_axis=0, tiled=True)  10.3 us
    all_to_all x1, starting transfers between devices, per_device(): lax.all_to_all(packed, 'tab', split_axis=0, concat_axis=0, tiled=True)  8.34 us
    unnamed x14, local copies, waits for them, and re-layouts  6.66 us
    all_to_all x1, starting transfers between devices, per_device(): lax.all_to_all(copies, 'tab', split_axis=0, concat_axis=0, tiled=True)  6 us
    pallas_call x1, Pallas kernels, per_device(): pl.pallas_call(functools.partial(pack_kernel, high=high, slots=slots), ou...  5.65 us
  transfers between devices with their start and end apart: 3, of which 3 were waited for; matrix products, arithmetic and copies ran while one was open for 6% of the time, Pallas kernels for 0%

profile of v2, /device:TPU:0, one launch (start us, length us, event | category | flops | bytes accessed | tf_op | source)
XLA Modules:
  0.0 156.1 jit_solution(1077739424707618621)
XLA Ops:
  0.6 0.7 broadcast_multiply_fusion
  1.4 1.0 add.35.rows_ref
  2.4 0.7 convert_element_type.9
  3.1 0.6 broadcast_in_dim.6.labels_ref
  3.7 5.6 %pack.1 = bf16[16,272,128]{2,1,0:T(8,128)(2,1)} custom-call(s32[128,1024]{1,0:T(8,128)} %bitcast.12, bf16[128,1024]{1,0:T(8,128)(2,1)} %bitcast.13, bf16[128,128]{1,0:T(8,128)(2,1)} %bitcast.14, f32[16,128]{1,0:T(8,128)} %broadcast_in_dim.6.labels_ref, s32[1024,1]{1,0:T(8,128)} %add.35.rows_ref), custom_call_target="tpu_custom_call" | custom-call | tf_op jit(solution)/shard_map/pack/pallas_call | solution.py:183
  9.4 8.3 %all-to-all-start = ((bf16[16,272,128]{2,1,0:T(8,128)(2,1)}), bf16[16,272,128]{2,1,0:T(8,128)(2,1)S(1)}, u32[]{:S(2)}, u32[]{:S(2)}) async-start(bf16[16,272,128]{2,1,0:T(8,128)(2,1)} %pack.1), calls=%async_computation | async-start | bytes 2228224 | tf_op jit(solution)/shard_map/all_to_all | solution.py:194
  17.7 4.6 %copy.15 = bf16[8,1536,128]{1,2,0:T(8,128)(2,1)} copy(bf16[8,1536,128]{2,1,0:T(8,128)(2,1)} %param.13) | data formatting | bytes 6291456 | tf_op args[4]
  22.4 21.0 %all-to-all-done.recv_ref.labels_ref = bf16[16,272,128]{2,1,0:T(8,128)(2,1)S(1)} async-done(((bf16[16,272,128]{2,1,0:T(8,128)(2,1)}), bf16[16,272,128]{2,1,0:T(8,128)(2,1)S(1)}, u32[]{:S(2)}, u32[]{:S(2)}) %all-to-all-start) | async-done | bytes 1114144 | tf_op jit(solution)/shard_map/all_to_all | solution.py:194
  43.4 1.0 copy-done
  44.4 71.3 %pool.1 = bf16[8,2048]{1,0:T(8,128)(2,1)} custom-call(bf16[16,272,128]{2,1,0:T(8,128)(2,1)} %copy-done, bf16[8,128,1536]{2,1,0:T(8,128)(2,1)} %bitcast.9), custom_call_target="tpu_custom_call" | custom-call | tf_op jit(solution)/shard_map/pool/pallas_call | solution.py:197
  115.7 1.6 %broadcast_in_dim.7 = bf16[16,8,2048]{2,1,0:T(8,128)(2,1)} broadcast(bf16[8,2048]{1,0:T(8,128)(2,1)} %pool.1), dimensions={1,2} | broadcast | bytes 557056 | tf_op jit(solution)/shard_map/broadcast_in_dim | solution.py:216
  117.3 6.0 %all-to-all-start.1 = ((bf16[16,8,2048]{2,1,0:T(8,128)(2,1)}), bf16[16,8,2048]{2,1,0:T(8,128)(2,1)S(1)}, u32[]{:S(2)}, u32[]{:S(2)}) async-start(bf16[16,8,2048]{2,1,0:T(8,128)(2,1)} %broadcast_in_dim.7), calls=%async_computation.1 | async-start | bytes 1048576 | tf_op jit(solution)/shard_map/all_to_all | solution.py:217
  123.3 1.1 copy.18.wide_ref
  124.4 1.0 copy.17.bias_ref
  125.4 0.8 copy.16
  126.2 0.6 fusion.place_ref
  126.9 10.3 %all-to-all-done.1 = bf16[16,8,2048]{2,1,0:T(8,128)(2,1)S(1)} async-done(((bf16[16,8,2048]{2,1,0:T(8,128)(2,1)}), bf16[16,8,2048]{2,1,0:T(8,128)(2,1)S(1)}, u32[]{:S(2)}, u32[]{:S(2)}) %all-to-all-start.1) | async-done | bytes 524320 | tf_op jit(solution)/shard_map/all_to_all | solution.py:217
  137.2 0.6 broadcast_in_dim.8.narrow_ref
  138.0 13.3 %top.1 = (f32[8,2048]{1,0:T(8,128)}, f32[144,1024]{1,0:T(8,128)}) custom-call(bf16[128,2048]{1,0:T(8,128)(2,1)} %bitcast.10, bf16[16,272,128]{2,1,0:T(8,128)(2,1)} %copy-done, bf16[128,128]{1,0:T(8,128)(2,1)} %fusion.place_ref, bf16[1024,128]{1,0:T(8,128)(2,1)} %bitcast.11, f32[1024,1]{1,0:T(8,128)} %copy.17.bias_ref, f32[1024,1]{1,0:T(8,128)} %copy.18.wide_ref, ...), custom_call_target="tpu_custom_call" | custom-call | tf_op jit(solution)/shard_map/top/pallas_call | solution.py:221
  151.3 0.7 dynamic-slice_reduce_fusion
  152.0 0.7 reshape.67
  152.7 0.8 collective-permute-done
  153.5 1.1 add.34
  154.6 0.8 slice.8
  (16 shorter events, 0.9 us)
Async XLA Ops:
  9.4 34.0 %all-to-all-start = ((bf16[16,272,128]{2,1,0:T(8,128)(2,1)}), bf16[16,272,128]{2,1,0:T(8,128)(2,1)S(1)}, u32[]{:S(2)}, u32[]{:S(2)}) async-start(bf16[16,272,128]{2,1,0:T(8,128)(2,1)} %pack.1), calls=%async_computation | async-start | bytes 2228224 | tf_op jit(solution)/shard_map/all_to_all | solution.py:194
  22.4 100.9 %copy-start.3 = (bf16[1024]{0:T(1024)(128)(2,1)S(1)}, bf16[1024]{0:T(1024)(128)(2,1)}, u32[]{:S(2)}) copy-start(bf16[1024]{0:T(1024)(128)(2,1)} %param.17) | copy-start | bytes 6148
  43.4 1.0 copy-start
  44.4 80.0 %copy-start.4 = (f32[1024]{0:T(1024)S(1)}, f32[1024]{0:T(1024)}, u32[]{:S(2)}) copy-start(f32[1024]{0:T(1024)} %param.16) | copy-start | bytes 12292
  44.4 81.0 %copy-start.2 = (bf16[128,1024]{1,0:T(8,128)(2,1)S(1)}, bf16[128,1024]{1,0:T(8,128)(2,1)}, u32[]{:S(2)}) copy-start(bf16[128,1024]{1,0:T(8,128)(2,1)} %param.15) | copy-start | bytes 786436
  44.4 81.8 %copy-start.5 = (s32[128]{0:T(128)S(1)}, s32[128]{0:T(128)}, u32[]{:S(2)}) copy-start(s32[128]{0:T(128)} %param.14) | copy-start | bytes 1540
  117.3 19.9 %all-to-all-start.1 = ((bf16[16,8,2048]{2,1,0:T(8,128)(2,1)}), bf16[16,8,2048]{2,1,0:T(8,128)(2,1)S(1)}, u32[]{:S(2)}, u32[]{:S(2)}) async-start(bf16[16,8,2048]{2,1,0:T(8,128)(2,1)} %broadcast_in_dim.7), calls=%async_computation.1 | async-start | bytes 1048576 | tf_op jit(solution)/shard_map/all_to_all | solution.py:217
  137.2 0.8 copy-start.1
  151.3 2.2 %collective-permute-start = (f32[144,1024]{1,0:T(8,128)}, f32[144,1024]{1,0:T(8,128)S(1)}, u32[]{:S(2)}, u32[]{:S(2)}) collective-permute-start(f32[144,1024]{1,0:T(8,128)} %get-tuple-element.6), channel_id=1, source_target_pairs={{0,16},{16,0},{1,17},{17,1},{2,18},{18,2},{3,19},{19,3},{4,20},{20... | collective-permute-start | bytes 1769480 | tf_op jit(solution)/shard_map/ppermute | solution.py:257
